TPU v7x, 32 devices: a whole 2x2x4 slice. The times are simulated.
32 devices in a mesh: section: 2 (over x), tp: 16 (over z, y, core).
Axes of the slice: x: 2, y: 2, z: 4, core: 2. Of those that a mesh axis runs over, the one named last changes fastest.
Arguments:
- states: float32 [2, 128, 4096], P('section', 'tp'), may hold values from -6 to 6
- text_embed: bfloat16 [1, 128, 4096], P(None, 'tp'), may hold values from -6 to 6
- visual_embed: bfloat16 [1, 128, 4096], P(None, 'tp'), may hold values from -6 to 6
- prefix_len: int32 [1, 4], replicated, may hold values from 1 to 31
- segment_ids: int32 [3, 128], replicated, may hold values from 0 to 3, never falling along the last dimension, each value on 1 to 64 neighbouring positions
- gain: float32 [2, 4096], P('section'), may hold values from 0.25 to 1.75
- w_query: bfloat16 [2, 4096, 2048], P('section', None, 'tp'), may hold values from -0.5625 to 0.5625
- w_keyval: bfloat16 [2, 4096, 2048], P('section', None, 'tp'), may hold values from -0.5625 to 0.5625
- w_out: bfloat16 [2, 2048, 4096], P('section', 'tp'), may hold values from -0.5 to 0.5
Outputs:
- section_out: float32 [2, 2, 128, 4096], P(None, 'section', 'tp')
All inputs are finite; a program needn't handle non-finite values.
Results may differ from a plain program's by a relative error of at most 0.028.
Values may be sent and summed in bfloat16 or wider, within the bound.
A program may use at most 64 MiB of HBM per device.

v0:
```python
import jax
import jax.numpy as jnp
from jax import lax
from jax.sharding import PartitionSpec as P

HEAD = 64
WINDOW = 2
norm_eps = 1e-05
rope_base = 500000.0


def shifted(block, axis, distance):
    devices = range(lax.axis_size(axis))
    route = [(i - distance, i) for i in devices if i - distance in devices]
    return lax.ppermute(block, axis, route)


def seg_offsets(seg_row):
    earlier = (seg_row[None, :] < seg_row[:, None]).astype(jnp.int32)
    first_pos = jnp.sum(earlier, axis=1)
    return jnp.arange(seg_row.shape[0], dtype=jnp.int32) - first_pos


def rotate(values, offsets):
    half_dim = values.shape[-1] // 2
    inv_freq = rope_base ** (-(jnp.arange(half_dim, dtype=jnp.float32) * 2.0) / values.shape[-1])
    angles = offsets.astype(jnp.float32)[:, None] * inv_freq[None, :]
    view_shape = (values.shape[0],) + (1,) * (values.ndim - 2) + (half_dim,)
    cosine = jnp.cos(angles).reshape(view_shape)
    sine_part = jnp.sin(angles).reshape(view_shape)
    front_half = values[..., :half_dim]
    back_half = values[..., half_dim:]
    return jnp.concatenate(
        [front_half * cosine - back_half * sine_part, back_half * cosine + front_half * sine_part],
        axis=-1,
    )


def rms_normed(rows, gain_row):
    scale = lax.rsqrt(jnp.mean(rows * rows, axis=-1, keepdims=True) + norm_eps)
    return rows * scale * gain_row


def body(states, text_embed, visual_embed, prefix_len, segment_ids, gain, w_query, w_keyval, w_out):
    section_pos = lax.axis_index("section")
    rank_pos = lax.axis_index("tp")
    section_count = lax.axis_size("section")
    shard_rows = states.shape[1]
    gain_row = gain[0]
    query_w = w_query[0]
    keyval_w = w_keyval[0]
    out_w = w_out[0]
    query_cols = query_w.shape[1]
    residual = states[0]
    outputs = []
    for step_num in range(WINDOW):
        if step_num > 0:
            arrived = shifted(residual.astype(jnp.bfloat16), "section", 1).astype(residual.dtype)
            batch_num = step_num - 1
            embed_seg_row = segment_ids[section_count + batch_num]
            offsets = seg_offsets(embed_seg_row)
            onehot = (
                embed_seg_row[:, None] == jnp.arange(prefix_len.shape[1], dtype=jnp.int32)[None, :]
            )
            prefix_cap = jnp.sum(jnp.where(onehot, prefix_len[batch_num][None, :], 0), axis=1)
            own_visual = lax.dynamic_slice_in_dim(
                offsets < prefix_cap, rank_pos * shard_rows, shard_rows, 0
            )
            residual = jnp.where(
                section_pos == 0,
                jnp.where(
                    own_visual[:, None], visual_embed[batch_num], text_embed[batch_num]
                ).astype(jnp.float32),
                arrived,
            )
        seg_row = lax.dynamic_index_in_dim(
            segment_ids, step_num - section_pos + section_count - 1, 0, keepdims=False
        )
        apply_normed = rms_normed(residual, gain_row).astype(jnp.bfloat16)
        normed = lax.all_gather(apply_normed, "tp", axis=0, tiled=True)
        mapped = jnp.concatenate(
            [
                jnp.dot(normed, query_w, preferred_element_type=jnp.float32),
                jnp.dot(normed, keyval_w, preferred_element_type=jnp.float32),
            ],
            axis=1,
        )
        total_rows = mapped.shape[0]
        apply_offsets = seg_offsets(seg_row)
        queries = rotate(
            mapped[:, :query_cols].reshape(total_rows, query_cols // HEAD, HEAD), apply_offsets
        ).astype(jnp.bfloat16)
        key_rows = rotate(mapped[:, query_cols : query_cols + HEAD], apply_offsets).astype(
            jnp.bfloat16
        )
        value_rows = mapped[:, query_cols + HEAD :].astype(jnp.bfloat16)
        scores = jnp.einsum(
            "qhd,kd->hqk", queries, key_rows, preferred_element_type=jnp.float32
        ) * HEAD ** (-0.5)
        position = jnp.arange(total_rows, dtype=jnp.int32)
        allowed = (seg_row[None, :] == seg_row[:, None]) & (position[None, :] <= position[:, None])
        scores = jnp.where(allowed[None], scores, -1e30)
        weights = jax.nn.softmax(scores, axis=-1).astype(jnp.bfloat16)
        mixed_heads = (
            jnp.einsum("hqk,kd->qhd", weights, value_rows, preferred_element_type=jnp.float32)
            .astype(jnp.bfloat16)
            .reshape(total_rows, query_cols)
        )
        residual = residual + lax.psum_scatter(
            jnp.dot(mixed_heads, out_w, preferred_element_type=jnp.float32).astype(jnp.bfloat16),
            "tp",
            scatter_dimension=0,
            tiled=True,
        ).astype(jnp.float32)
        outputs.append(residual)
    return jnp.stack(outputs)[:, None]


def solution(mesh):
    return jax.shard_map(
        body,
        mesh=mesh,
        in_specs=(
            P("section", "tp", None),
            P(None, "tp", None),
            P(None, "tp", None),
            P(),
            P(),
            P("section", None),
            P("section", None, "tp"),
            P("section", None, "tp"),
            P("section", "tp", None),
        ),
        out_specs=P(None, "section", "tp", None),
        check_vma=False,
    )
```

profile of v0, /device:TPU:0, one launch (start us, length us, event | category | flops | bytes accessed | tf_op | source)
XLA Modules:
  0.0 227.0 jit_solution(10462846901884635893)
XLA Ops:
  6.5 1.1 fusion.20
  7.7 1.6 fusion.22
  9.4 1.6 copy.19
  11.0 0.6 slice_bitcast_fusion
  11.8 38.3 %all-gather.3.cloned.1.call-done = bf16[128,4096]{1,0:T(8,128)(2,1)} async-done(((bf16[8,4096]{1,0:T(8,128)(2,1)}), bf16[128,4096]{1,0:T(8,128)(2,1)}) %all-gather.3.cloned.1.call-update) | async-done | bytes 1048592 | tf_op jit(solution)/shard_map/all_gather | solution.py:80
  50.1 1.8 fusion.18
  53.3 1.5 convolution_convert_fusion.1
  54.9 0.6 copy-done.11
  55.4 0.7 convert_reduce_fusion.1
  56.1 0.7 select_reduce_fusion
  56.8 54.8 %reduce-scatter.3.cloned.1.call-done = bf16[8,4096]{1,0:T(8,128)(2,1)} async-done(((bf16[128,4096]{1,0:T(8,128)(2,1)}), bf16[8,4096]{1,0:T(8,128)(2,1)}) %reduce-scatter.3.cloned.1.call-update) | async-done | bytes 65552 | tf_op jit(solution)/shard_map/reduce_scatter | solution.py:109
  111.6 1.5 fusion.24
  113.1 3.3 %collective-permute-start = (bf16[8,4096]{1,0:T(8,128)(2,1)}, bf16[8,4096]{1,0:T(8,128)(2,1)S(1)}, u32[]{:S(2)}, u32[]{:S(2)}) collective-permute-start(bf16[8,4096]{1,0:T(8,128)(2,1)} %get-tuple-element.8), channel_id=1, source_target_pairs={{0,16},{1,17},{2,18},{3,19},{4,20},{5,21},{6,22},{7,23},{8,24},{9,... | collective-permute-start | bytes 196616 | tf_op jit(solution)/shard_map/ppermute | solution.py:15
  116.4 0.7 subtract_compare_fusion
  117.2 1.4 collective-permute-done
  118.9 0.7 multiply_convert_fusion
  119.7 0.8 convert_reduce_fusion
  120.5 0.8 fusion.25
  121.3 36.1 %all-gather.5.cloned.1.call-done = bf16[128,4096]{1,0:T(8,128)(2,1)} async-done(((bf16[8,4096]{1,0:T(8,128)(2,1)}), bf16[128,4096]{1,0:T(8,128)(2,1)}) %all-gather.5.cloned.1.call-update) | async-done | bytes 1048592 | tf_op jit(solution)/shard_map/all_gather | solution.py:80
  157.4 1.8 fusion.16
  160.6 1.5 convolution_convert_fusion
  162.1 56.8 %reduce-scatter.5.cloned.1.call-done = bf16[8,4096]{1,0:T(8,128)(2,1)} async-done(((bf16[128,4096]{1,0:T(8,128)(2,1)}), bf16[8,4096]{1,0:T(8,128)(2,1)}) %reduce-scatter.5.cloned.1.call-update) | async-done | bytes 65552 | tf_op jit(solution)/shard_map/reduce_scatter | solution.py:109
  218.9 0.9 add_bitcast_fusion
  219.7 0.7 maximum_bitcast_fusion
  (54 shorter events, 3.4 us)
Async XLA Ops:
  6.5 46.8 %copy-start = (bf16[1,128,4096]{2,1,0:T(8,128)(2,1)S(1)}, bf16[1,128,4096]{2,1,0:T(8,128)(2,1)}, u32[]{:S(2)}) copy-start(bf16[1,128,4096]{2,1,0:T(8,128)(2,1)} %param.17) | copy-start | bytes 3145732
  6.5 43.6 %all-gather.3.cloned.1.call-start = ((), (), s32[]{:S(2)}) async-start(), calls=%async_computation.2 | async-start | bytes 1114112 | tf_op jit(solution)/shard_map/all_gather | solution.py:80
  9.3 102.3 %reduce-scatter.3.cloned.1.call-start = ((), (), s32[]{:S(2)}) async-start(), calls=%async_computation.3 | async-start | bytes 1114112 | tf_op jit(solution)/shard_map/reduce_scatter | solution.py:109
  9.4 1.6 copy-start.10
  9.4 40.7 %copy-start.1 = (bf16[1,4096,128]{2,1,0:T(8,128)(2,1)S(1)}, bf16[1,4096,128]{2,1,0:T(8,128)(2,1)}, u32[]{:S(2)}) copy-start(bf16[1,4096,128]{2,1,0:T(8,128)(2,1)} %param.16) | copy-start | bytes 3145732
  11.0 40.9 %copy-start.8 = (f32[32]{0:T(128)}, f32[32]{0:T(128)S(1)}, u32[]{:S(2)}) copy-start(f32[32]{0:T(128)S(1)} %multiply_power_fusion) | copy-start | bytes 388
  50.1 2.0 copy-start.2
  54.8 0.7 copy-start.11
  54.8 1.4 copy-start.12
  54.8 56.9 %copy-start.4 = (f32[1,8,4096]{2,1,0:T(8,128)S(1)}, f32[1,8,4096]{2,1,0:T(8,128)}, u32[]{:S(2)}) copy-start(f32[1,8,4096]{2,1,0:T(8,128)} %param.9) | copy-start | bytes 393220
  54.8 63.8 %copy-start.5 = (bf16[1,8,4096]{2,1,0:T(8,128)(2,1)S(1)}, bf16[1,8,4096]{2,1,0:T(8,128)(2,1)}, u32[]{:S(2)}) copy-start(bf16[1,8,4096]{2,1,0:T(8,128)(2,1)} %param.10) | copy-start | bytes 196612
  54.8 63.8 %copy-start.6 = (bf16[1,8,4096]{2,1,0:T(8,128)(2,1)S(1)}, bf16[1,8,4096]{2,1,0:T(8,128)(2,1)}, u32[]{:S(2)}) copy-start(bf16[1,8,4096]{2,1,0:T(8,128)(2,1)} %param.11) | copy-start | bytes 196612
  54.8 64.1 %copy-start.7 = (f32[1,4096]{1,0:T(1,128)S(1)}, f32[1,4096]{1,0:T(1,128)}, u32[]{:S(2)}) copy-start(f32[1,4096]{1,0:T(1,128)} %param.14) | copy-start | bytes 49156
  54.8 102.6 %all-gather.5.cloned.1.call-start = ((), (), s32[]{:S(2)}) async-start(), calls=%async_computation.4 | async-start | bytes 1114112 | tf_op jit(solution)/shard_map/all_gather | solution.py:80
  113.1 5.5 %collective-permute-start = (bf16[8,4096]{1,0:T(8,128)(2,1)}, bf16[8,4096]{1,0:T(8,128)(2,1)S(1)}, u32[]{:S(2)}, u32[]{:S(2)}) collective-permute-start(bf16[8,4096]{1,0:T(8,128)(2,1)} %get-tuple-element.8), channel_id=1, source_target_pairs={{0,16},{1,17},{2,18},{3,19},{4,20},{5,21},{6,22},{7,23},{8,24},{9,... | collective-permute-start | bytes 196616 | tf_op jit(solution)/shard_map/ppermute | solution.py:15
  119.6 99.2 %reduce-scatter.5.cloned.1.call-start = ((), (), s32[]{:S(2)}) async-start(), calls=%async_computation.5 | async-start | bytes 1114112 | tf_op jit(solution)/shard_map/reduce_scatter | solution.py:109
  121.3 37.9 %copy-start.9 = (f32[32]{0:T(128)S(1)}, f32[32]{0:T(128)}, u32[]{:S(2)}) copy-start(f32[32]{0:T(128)} %copy-done.8) | copy-start | bytes 388
  157.4 2.0 copy-start.3
Sparse Core Ops, SparseCore 0:
  9.5 40.5 all-gather.2
  54.9 56.6 reduce-scatter.2
  119.7 37.6 all-gather.4
  162.2 56.5 reduce-scatter.4
where the time goes:
time: 227 us
  waiting for transfers between devices  187 us (82%)
  between operations  13.3 us (6%)
  other arithmetic  11 us (5%)
  matrix products  8.88 us (4%)
  starting transfers between devices  3.4 us (1%)
  local copies, waits for them, and re-layouts  2.86 us (1%)
    reduce_scatter x2, waiting for transfers between devices, body(): lax.psum_scatter(jnp.dot(mixed_heads, out_w, preferred_element_type=jnp.f...  112 us
    all_gather x2, waiting for transfers between devices, body(): normed = lax.all_gather(apply_normed, 'tp', axis=0, tiled=True)  74.3 us
  transfers between devices with their start and end apart: 5, of which 5 were waited for; matrix products, arithmetic and copies ran while one was open for 3% of the time, Pallas kernels for 0%

commit v1 on v0

--- a/solution.py
+++ b/solution.py
@@ -77,7 +77,14 @@
             segment_ids, step_num - section_pos + section_count - 1, 0, keepdims=False
         )
         apply_normed = rms_normed(residual, gain_row).astype(jnp.bfloat16)
-        normed = lax.all_gather(apply_normed, "tp", axis=0, tiled=True)
+        ring = [apply_normed]
+        for hop in range(15):
+            ring.append(lax.ppermute(ring[-1], "tp", [(dev, (dev + 1) % 16) for dev in range(16)]))
+        normed = jnp.roll(
+            jnp.concatenate(ring[::-1], axis=0),
+            (lax.axis_index("tp") + 1) * ring[0].shape[0],
+            axis=0,
+        )
         mapped = jnp.concatenate(
             [
                 jnp.dot(normed, query_w, preferred_element_type=jnp.float32),

time: 227 us -> 337 us (1.48)
  waiting for transfers between devices: 187 us -> 302 us
  other arithmetic: 11 us -> 5.98 us
    ppermute x0 -> x30, waiting for transfers between devices: none -> 189 us  [body(): lax.ppermute(ring[-1], 'tp', [(dev, (dev + 1) % 16) for dev in range(16)])]
    all_gather x2 -> x0, waiting for transfers between devices: 74.3 us -> none  [body(): normed = lax.all_gather(apply_normed, 'tp', axis=0, tiled=True)]
  transfers between devices with their start and end apart: 5 -> 33, of which waited for: 5 -> 33; matrix products, arithmetic and copies ran while one was open for 3% -> 1% of each run, Pallas kernels for 0% -> 0%
where the time goes in v1:
time: 337 us
  waiting for transfers between devices  302 us (90%)
  between operations  13.9 us (4%)
  matrix products  7.3 us (2%)
  other arithmetic  5.98 us (2%)
  starting transfers between devices  4.17 us (1%)
  local copies, waits for them, and re-layouts  3.91 us (1%)
    ppermute x30, waiting for transfers between devices, body(): lax.ppermute(ring[-1], 'tp', [(dev, (dev + 1) % 16) for dev in range(16)])  189 us
    reduce_scatter x2, waiting for transfers between devices, body(): lax.psum_scatter(jnp.dot(mixed_heads, out_w, preferred_element_type=jnp.f...  111 us
  transfers between devices with their start and end apart: 33, of which 33 were waited for; matrix products, arithmetic and copies ran while one was open for 1% of the time, Pallas kernels for 0%

profile of v1, /device:TPU:0, one launch (start us, length us, event | category | flops | bytes accessed | tf_op | source)
XLA Modules:
  0.0 337.0 jit_solution(17197074370112051363)
XLA Ops:
  9.2 6.9 %collective-permute-done = bf16[8,4096]{1,0:T(8,128)(2,1)S(1)} collective-permute-done((bf16[8,4096]{1,0:T(8,128)(2,1)S(1)}, bf16[8,4096]{1,0:T(8,128)(2,1)S(1)}, u32[]{:S(2)}, u32[]{:S(2)}) %collective-permute-start) | collective-permute-done | bytes 65568 | tf_op jit(solution)/shard_map/ppermute | solution.py:82
  16.2 6.4 %collective-permute-done.1 = bf16[8,4096]{1,0:T(8,128)(2,1)S(1)} collective-permute-done((bf16[8,4096]{1,0:T(8,128)(2,1)S(1)}, bf16[8,4096]{1,0:T(8,128)(2,1)S(1)}, u32[]{:S(2)}, u32[]{:S(2)}) %collective-permute-start.1) | collective-permute-done | bytes 65568 | tf_op jit(solution)/shard_map/ppermute | solution.py:82
  22.6 6.4 %collective-permute-done.2 = bf16[8,4096]{1,0:T(8,128)(2,1)S(1)} collective-permute-done((bf16[8,4096]{1,0:T(8,128)(2,1)S(1)}, bf16[8,4096]{1,0:T(8,128)(2,1)S(1)}, u32[]{:S(2)}, u32[]{:S(2)}) %collective-permute-start.2) | collective-permute-done | bytes 65568 | tf_op jit(solution)/shard_map/ppermute | solution.py:82
  28.9 6.4 %collective-permute-done.3 = bf16[8,4096]{1,0:T(8,128)(2,1)S(1)} collective-permute-done((bf16[8,4096]{1,0:T(8,128)(2,1)S(1)}, bf16[8,4096]{1,0:T(8,128)(2,1)S(1)}, u32[]{:S(2)}, u32[]{:S(2)}) %collective-permute-start.3) | collective-permute-done | bytes 65568 | tf_op jit(solution)/shard_map/ppermute | solution.py:82
  35.3 6.4 %collective-permute-done.4 = bf16[8,4096]{1,0:T(8,128)(2,1)S(1)} collective-permute-done((bf16[8,4096]{1,0:T(8,128)(2,1)S(1)}, bf16[8,4096]{1,0:T(8,128)(2,1)S(1)}, u32[]{:S(2)}, u32[]{:S(2)}) %collective-permute-start.4) | collective-permute-done | bytes 65568 | tf_op jit(solution)/shard_map/ppermute | solution.py:82
  41.7 6.4 %collective-permute-done.5 = bf16[8,4096]{1,0:T(8,128)(2,1)S(1)} collective-permute-done((bf16[8,4096]{1,0:T(8,128)(2,1)S(1)}, bf16[8,4096]{1,0:T(8,128)(2,1)S(1)}, u32[]{:S(2)}, u32[]{:S(2)}) %collective-permute-start.5) | collective-permute-done | bytes 65568 | tf_op jit(solution)/shard_map/ppermute | solution.py:82
  48.1 6.4 %collective-permute-done.6 = bf16[8,4096]{1,0:T(8,128)(2,1)S(1)} collective-permute-done((bf16[8,4096]{1,0:T(8,128)(2,1)S(1)}, bf16[8,4096]{1,0:T(8,128)(2,1)S(1)}, u32[]{:S(2)}, u32[]{:S(2)}) %collective-permute-start.6) | collective-permute-done | bytes 65568 | tf_op jit(solution)/shard_map/ppermute | solution.py:82
  54.5 6.4 %collective-permute-done.7 = bf16[8,4096]{1,0:T(8,128)(2,1)S(1)} collective-permute-done((bf16[8,4096]{1,0:T(8,128)(2,1)S(1)}, bf16[8,4096]{1,0:T(8,128)(2,1)S(1)}, u32[]{:S(2)}, u32[]{:S(2)}) %collective-permute-start.7) | collective-permute-done | bytes 65568 | tf_op jit(solution)/shard_map/ppermute | solution.py:82
  60.9 6.4 %collective-permute-done.8 = bf16[8,4096]{1,0:T(8,128)(2,1)S(1)} collective-permute-done((bf16[8,4096]{1,0:T(8,128)(2,1)S(1)}, bf16[8,4096]{1,0:T(8,128)(2,1)S(1)}, u32[]{:S(2)}, u32[]{:S(2)}) %collective-permute-start.8) | collective-permute-done | bytes 65568 | tf_op jit(solution)/shard_map/ppermute | solution.py:82
  67.3 6.4 %collective-permute-done.9 = bf16[8,4096]{1,0:T(8,128)(2,1)S(1)} collective-permute-done((bf16[8,4096]{1,0:T(8,128)(2,1)S(1)}, bf16[8,4096]{1,0:T(8,128)(2,1)S(1)}, u32[]{:S(2)}, u32[]{:S(2)}) %collective-permute-start.9) | collective-permute-done | bytes 65568 | tf_op jit(solution)/shard_map/ppermute | solution.py:82
  111.4 54.7 %reduce-scatter.3.cloned.1.call-done = bf16[8,4096]{1,0:T(8,128)(2,1)} async-done(((bf16[128,4096]{1,0:T(8,128)(2,1)}), bf16[8,4096]{1,0:T(8,128)(2,1)}) %reduce-scatter.3.cloned.1.call-update) | async-done | bytes 65552 | tf_op jit(solution)/shard_map/reduce_scatter | solution.py:116
  172.7 6.4 %collective-permute-done.16 = bf16[8,4096]{1,0:T(8,128)(2,1)S(1)} collective-permute-done((bf16[8,4096]{1,0:T(8,128)(2,1)S(1)}, bf16[8,4096]{1,0:T(8,128)(2,1)S(1)}, u32[]{:S(2)}, u32[]{:S(2)}) %collective-permute-start.16) | collective-permute-done | bytes 65568 | tf_op jit(solution)/shard_map/ppermute | solution.py:82
  179.1 6.4 %collective-permute-done.17 = bf16[8,4096]{1,0:T(8,128)(2,1)S(1)} collective-permute-done((bf16[8,4096]{1,0:T(8,128)(2,1)S(1)}, bf16[8,4096]{1,0:T(8,128)(2,1)S(1)}, u32[]{:S(2)}, u32[]{:S(2)}) %collective-permute-start.17) | collective-permute-done | bytes 65568 | tf_op jit(solution)/shard_map/ppermute | solution.py:82
  185.5 6.4 %collective-permute-done.18 = bf16[8,4096]{1,0:T(8,128)(2,1)S(1)} collective-permute-done((bf16[8,4096]{1,0:T(8,128)(2,1)S(1)}, bf16[8,4096]{1,0:T(8,128)(2,1)S(1)}, u32[]{:S(2)}, u32[]{:S(2)}) %collective-permute-start.18) | collective-permute-done | bytes 65568 | tf_op jit(solution)/shard_map/ppermute | solution.py:82
  191.9 6.4 %collective-permute-done.19 = bf16[8,4096]{1,0:T(8,128)(2,1)S(1)} collective-permute-done((bf16[8,4096]{1,0:T(8,128)(2,1)S(1)}, bf16[8,4096]{1,0:T(8,128)(2,1)S(1)}, u32[]{:S(2)}, u32[]{:S(2)}) %collective-permute-start.19) | collective-permute-done | bytes 65568 | tf_op jit(solution)/shard_map/ppermute | solution.py:82
  198.3 6.4 %collective-permute-done.20 = bf16[8,4096]{1,0:T(8,128)(2,1)S(1)} collective-permute-done((bf16[8,4096]{1,0:T(8,128)(2,1)S(1)}, bf16[8,4096]{1,0:T(8,128)(2,1)S(1)}, u32[]{:S(2)}, u32[]{:S(2)}) %collective-permute-start.20) | collective-permute-done | bytes 65568 | tf_op jit(solution)/shard_map/ppermute | solution.py:82
  204.6 6.4 %collective-permute-done.21 = bf16[8,4096]{1,0:T(8,128)(2,1)S(1)} collective-permute-done((bf16[8,4096]{1,0:T(8,128)(2,1)S(1)}, bf16[8,4096]{1,0:T(8,128)(2,1)S(1)}, u32[]{:S(2)}, u32[]{:S(2)}) %collective-permute-start.21) | collective-permute-done | bytes 65568 | tf_op jit(solution)/shard_map/ppermute | solution.py:82
  211.0 6.4 %collective-permute-done.22 = bf16[8,4096]{1,0:T(8,128)(2,1)S(1)} collective-permute-done((bf16[8,4096]{1,0:T(8,128)(2,1)S(1)}, bf16[8,4096]{1,0:T(8,128)(2,1)S(1)}, u32[]{:S(2)}, u32[]{:S(2)}) %collective-permute-start.22) | collective-permute-done | bytes 65568 | tf_op jit(solution)/shard_map/ppermute | solution.py:82
  217.4 6.4 %collective-permute-done.23 = bf16[8,4096]{1,0:T(8,128)(2,1)S(1)} collective-permute-done((bf16[8,4096]{1,0:T(8,128)(2,1)S(1)}, bf16[8,4096]{1,0:T(8,128)(2,1)S(1)}, u32[]{:S(2)}, u32[]{:S(2)}) %collective-permute-start.23) | collective-permute-done | bytes 65568 | tf_op jit(solution)/shard_map/ppermute | solution.py:82
  223.8 6.4 %collective-permute-done.24 = bf16[8,4096]{1,0:T(8,128)(2,1)S(1)} collective-permute-done((bf16[8,4096]{1,0:T(8,128)(2,1)S(1)}, bf16[8,4096]{1,0:T(8,128)(2,1)S(1)}, u32[]{:S(2)}, u32[]{:S(2)}) %collective-permute-start.24) | collective-permute-done | bytes 65568 | tf_op jit(solution)/shard_map/ppermute | solution.py:82
  230.2 6.4 %collective-permute-done.25 = bf16[8,4096]{1,0:T(8,128)(2,1)S(1)} collective-permute-done((bf16[8,4096]{1,0:T(8,128)(2,1)S(1)}, bf16[8,4096]{1,0:T(8,128)(2,1)S(1)}, u32[]{:S(2)}, u32[]{:S(2)}) %collective-permute-start.25) | collective-permute-done | bytes 65568 | tf_op jit(solution)/shard_map/ppermute | solution.py:82
  236.6 6.4 %collective-permute-done.26 = bf16[8,4096]{1,0:T(8,128)(2,1)S(1)} collective-permute-done((bf16[8,4096]{1,0:T(8,128)(2,1)S(1)}, bf16[8,4096]{1,0:T(8,128)(2,1)S(1)}, u32[]{:S(2)}, u32[]{:S(2)}) %collective-permute-start.26) | collective-permute-done | bytes 65568 | tf_op jit(solution)/shard_map/ppermute | solution.py:82
  243.0 6.4 %collective-permute-done.27 = bf16[8,4096]{1,0:T(8,128)(2,1)S(1)} collective-permute-done((bf16[8,4096]{1,0:T(8,128)(2,1)S(1)}, bf16[8,4096]{1,0:T(8,128)(2,1)S(1)}, u32[]{:S(2)}, u32[]{:S(2)}) %collective-permute-start.27) | collective-permute-done | bytes 65568 | tf_op jit(solution)/shard_map/ppermute | solution.py:82
  272.6 55.9 %reduce-scatter.5.cloned.1.call-done = bf16[8,4096]{1,0:T(8,128)(2,1)} async-done(((bf16[128,4096]{1,0:T(8,128)(2,1)}), bf16[8,4096]{1,0:T(8,128)(2,1)}) %reduce-scatter.5.cloned.1.call-update) | async-done | bytes 65552 | tf_op jit(solution)/shard_map/reduce_scatter | solution.py:116
  (130 shorter events, 71.5 us)
Async XLA Ops:
  6.5 159.6 %reduce-scatter.3.cloned.1.call-start = ((), (), s32[]{:S(2)}) async-start(), calls=%async_computation.2 | async-start | bytes 1114112 | tf_op jit(solution)/shard_map/reduce_scatter | solution.py:116
  8.7 7.5 %collective-permute-start = (bf16[8,4096]{1,0:T(8,128)(2,1)S(1)}, bf16[8,4096]{1,0:T(8,128)(2,1)S(1)}, u32[]{:S(2)}, u32[]{:S(2)}) collective-permute-start(bf16[8,4096]{1,0:T(8,128)(2,1)S(1)} %fusion.24), channel_id=1, source_target_pairs={{0,1},{1,2},{2,3},{3,4},{4,5},{5,6},{6,7},{7,8},{8,9},{9,10},{10,1... | collective-permute-start | bytes 196616 | tf_op jit(solution)/shard_map/ppermute | solution.py:82
  16.2 6.4 %collective-permute-start.1 = (bf16[8,4096]{1,0:T(8,128)(2,1)S(1)}, bf16[8,4096]{1,0:T(8,128)(2,1)S(1)}, u32[]{:S(2)}, u32[]{:S(2)}) collective-permute-start(bf16[8,4096]{1,0:T(8,128)(2,1)S(1)} %collective-permute-done), channel_id=1, source_target_pairs={{0,1},{1,2},{2,3},{3,4},{4,5},{5,6},{6,7},{7,8},{8,9},{9,10},{10,1... | collective-permute-start | bytes 196616 | tf_op jit(solution)/shard_map/ppermute | solution.py:82
  22.6 6.4 %collective-permute-start.2 = (bf16[8,4096]{1,0:T(8,128)(2,1)S(1)}, bf16[8,4096]{1,0:T(8,128)(2,1)S(1)}, u32[]{:S(2)}, u32[]{:S(2)}) collective-permute-start(bf16[8,4096]{1,0:T(8,128)(2,1)S(1)} %collective-permute-done.1), channel_id=1, source_target_pairs={{0,1},{1,2},{2,3},{3,4},{4,5},{5,6},{6,7},{7,8},{8,9},{9,10},{10,1... | collective-permute-start | bytes 196616 | tf_op jit(solution)/shard_map/ppermute | solution.py:82
  28.9 6.4 %collective-permute-start.3 = (bf16[8,4096]{1,0:T(8,128)(2,1)S(1)}, bf16[8,4096]{1,0:T(8,128)(2,1)S(1)}, u32[]{:S(2)}, u32[]{:S(2)}) collective-permute-start(bf16[8,4096]{1,0:T(8,128)(2,1)S(1)} %collective-permute-done.2), channel_id=1, source_target_pairs={{0,1},{1,2},{2,3},{3,4},{4,5},{5,6},{6,7},{7,8},{8,9},{9,10},{10,1... | collective-permute-start | bytes 196616 | tf_op jit(solution)/shard_map/ppermute | solution.py:82
  35.3 6.4 %collective-permute-start.4 = (bf16[8,4096]{1,0:T(8,128)(2,1)S(1)}, bf16[8,4096]{1,0:T(8,128)(2,1)S(1)}, u32[]{:S(2)}, u32[]{:S(2)}) collective-permute-start(bf16[8,4096]{1,0:T(8,128)(2,1)S(1)} %collective-permute-done.3), channel_id=1, source_target_pairs={{0,1},{1,2},{2,3},{3,4},{4,5},{5,6},{6,7},{7,8},{8,9},{9,10},{10,1... | collective-permute-start | bytes 196616 | tf_op jit(solution)/shard_map/ppermute | solution.py:82
  41.7 6.4 %collective-permute-start.5 = (bf16[8,4096]{1,0:T(8,128)(2,1)S(1)}, bf16[8,4096]{1,0:T(8,128)(2,1)S(1)}, u32[]{:S(2)}, u32[]{:S(2)}) collective-permute-start(bf16[8,4096]{1,0:T(8,128)(2,1)S(1)} %collective-permute-done.4), channel_id=1, source_target_pairs={{0,1},{1,2},{2,3},{3,4},{4,5},{5,6},{6,7},{7,8},{8,9},{9,10},{10,1... | collective-permute-start | bytes 196616 | tf_op jit(solution)/shard_map/ppermute | solution.py:82
  48.1 6.4 %collective-permute-start.6 = (bf16[8,4096]{1,0:T(8,128)(2,1)S(1)}, bf16[8,4096]{1,0:T(8,128)(2,1)S(1)}, u32[]{:S(2)}, u32[]{:S(2)}) collective-permute-start(bf16[8,4096]{1,0:T(8,128)(2,1)S(1)} %collective-permute-done.5), channel_id=1, source_target_pairs={{0,1},{1,2},{2,3},{3,4},{4,5},{5,6},{6,7},{7,8},{8,9},{9,10},{10,1... | collective-permute-start | bytes 196616 | tf_op jit(solution)/shard_map/ppermute | solution.py:82
  54.5 6.4 %collective-permute-start.7 = (bf16[8,4096]{1,0:T(8,128)(2,1)S(1)}, bf16[8,4096]{1,0:T(8,128)(2,1)S(1)}, u32[]{:S(2)}, u32[]{:S(2)}) collective-permute-start(bf16[8,4096]{1,0:T(8,128)(2,1)S(1)} %collective-permute-done.6), channel_id=1, source_target_pairs={{0,1},{1,2},{2,3},{3,4},{4,5},{5,6},{6,7},{7,8},{8,9},{9,10},{10,1... | collective-permute-start | bytes 196616 | tf_op jit(solution)/shard_map/ppermute | solution.py:82
  60.9 6.4 %collective-permute-start.8 = (bf16[8,4096]{1,0:T(8,128)(2,1)S(1)}, bf16[8,4096]{1,0:T(8,128)(2,1)S(1)}, u32[]{:S(2)}, u32[]{:S(2)}) collective-permute-start(bf16[8,4096]{1,0:T(8,128)(2,1)S(1)} %collective-permute-done.7), channel_id=1, source_target_pairs={{0,1},{1,2},{2,3},{3,4},{4,5},{5,6},{6,7},{7,8},{8,9},{9,10},{10,1... | collective-permute-start | bytes 196616 | tf_op jit(solution)/shard_map/ppermute | solution.py:82
  67.3 6.4 %collective-permute-start.9 = (bf16[8,4096]{1,0:T(8,128)(2,1)S(1)}, bf16[8,4096]{1,0:T(8,128)(2,1)S(1)}, u32[]{:S(2)}, u32[]{:S(2)}) collective-permute-start(bf16[8,4096]{1,0:T(8,128)(2,1)S(1)} %collective-permute-done.8), channel_id=1, source_target_pairs={{0,1},{1,2},{2,3},{3,4},{4,5},{5,6},{6,7},{7,8},{8,9},{9,10},{10,1... | collective-permute-start | bytes 196616 | tf_op jit(solution)/shard_map/ppermute | solution.py:82
  73.7 6.4 %collective-permute-start.10 = (bf16[8,4096]{1,0:T(8,128)(2,1)S(1)}, bf16[8,4096]{1,0:T(8,128)(2,1)S(1)}, u32[]{:S(2)}, u32[]{:S(2)}) collective-permute-start(bf16[8,4096]{1,0:T(8,128)(2,1)S(1)} %collective-permute-done.9), channel_id=1, source_target_pairs={{0,1},{1,2},{2,3},{3,4},{4,5},{5,6},{6,7},{7,8},{8,9},{9,10},{10,1... | collective-permute-start | bytes 196616 | tf_op jit(solution)/shard_map/ppermute | solution.py:82
  99.2 6.4 %collective-permute-start.14 = (bf16[8,4096]{1,0:T(8,128)(2,1)S(1)}, bf16[8,4096]{1,0:T(8,128)(2,1)S(1)}, u32[]{:S(2)}, u32[]{:S(2)}) collective-permute-start(bf16[8,4096]{1,0:T(8,128)(2,1)S(1)} %collective-permute-done.13), channel_id=1, source_target_pairs={{0,1},{1,2},{2,3},{3,4},{4,5},{5,6},{6,7},{7,8},{8,9},{9,10},{10,1... | collective-permute-start | bytes 196616 | tf_op jit(solution)/shard_map/ppermute | solution.py:82
  110.7 217.8 %reduce-scatter.5.cloned.1.call-start = ((), (), s32[]{:S(2)}) async-start(), calls=%async_computation.3 | async-start | bytes 1114112 | tf_op jit(solution)/shard_map/reduce_scatter | solution.py:116
  172.6 6.4 %collective-permute-start.16 = (bf16[8,4096]{1,0:T(8,128)(2,1)S(1)}, bf16[8,4096]{1,0:T(8,128)(2,1)S(1)}, u32[]{:S(2)}, u32[]{:S(2)}) collective-permute-start(bf16[8,4096]{1,0:T(8,128)(2,1)S(1)} %multiply_convert_fusion), channel_id=1, source_target_pairs={{0,1},{1,2},{2,3},{3,4},{4,5},{5,6},{6,7},{7,8},{8,9},{9,10},{10,1... | collective-permute-start | bytes 196616 | tf_op jit(solution)/shard_map/ppermute | solution.py:82
  179.1 6.4 %collective-permute-start.17 = (bf16[8,4096]{1,0:T(8,128)(2,1)S(1)}, bf16[8,4096]{1,0:T(8,128)(2,1)S(1)}, u32[]{:S(2)}, u32[]{:S(2)}) collective-permute-start(bf16[8,4096]{1,0:T(8,128)(2,1)S(1)} %collective-permute-done.16), channel_id=1, source_target_pairs={{0,1},{1,2},{2,3},{3,4},{4,5},{5,6},{6,7},{7,8},{8,9},{9,10},{10,1... | collective-permute-start | bytes 196616 | tf_op jit(solution)/shard_map/ppermute | solution.py:82
  185.5 6.4 %collective-permute-start.18 = (bf16[8,4096]{1,0:T(8,128)(2,1)S(1)}, bf16[8,4096]{1,0:T(8,128)(2,1)S(1)}, u32[]{:S(2)}, u32[]{:S(2)}) collective-permute-start(bf16[8,4096]{1,0:T(8,128)(2,1)S(1)} %collective-permute-done.17), channel_id=1, source_target_pairs={{0,1},{1,2},{2,3},{3,4},{4,5},{5,6},{6,7},{7,8},{8,9},{9,10},{10,1... | collective-permute-start | bytes 196616 | tf_op jit(solution)/shard_map/ppermute | solution.py:82
  191.9 6.4 %collective-permute-start.19 = (bf16[8,4096]{1,0:T(8,128)(2,1)S(1)}, bf16[8,4096]{1,0:T(8,128)(2,1)S(1)}, u32[]{:S(2)}, u32[]{:S(2)}) collective-permute-start(bf16[8,4096]{1,0:T(8,128)(2,1)S(1)} %collective-permute-done.18), channel_id=1, source_target_pairs={{0,1},{1,2},{2,3},{3,4},{4,5},{5,6},{6,7},{7,8},{8,9},{9,10},{10,1... | collective-permute-start | bytes 196616 | tf_op jit(solution)/shard_map/ppermute | solution.py:82
  198.3 6.4 %collective-permute-start.20 = (bf16[8,4096]{1,0:T(8,128)(2,1)S(1)}, bf16[8,4096]{1,0:T(8,128)(2,1)S(1)}, u32[]{:S(2)}, u32[]{:S(2)}) collective-permute-start(bf16[8,4096]{1,0:T(8,128)(2,1)S(1)} %collective-permute-done.19), channel_id=1, source_target_pairs={{0,1},{1,2},{2,3},{3,4},{4,5},{5,6},{6,7},{7,8},{8,9},{9,10},{10,1... | collective-permute-start | bytes 196616 | tf_op jit(solution)/shard_map/ppermute | solution.py:82
  236.6 6.4 %collective-permute-start.26 = (bf16[8,4096]{1,0:T(8,128)(2,1)S(1)}, bf16[8,4096]{1,0:T(8,128)(2,1)S(1)}, u32[]{:S(2)}, u32[]{:S(2)}) collective-permute-start(bf16[8,4096]{1,0:T(8,128)(2,1)S(1)} %collective-permute-done.25), channel_id=1, source_target_pairs={{0,1},{1,2},{2,3},{3,4},{4,5},{5,6},{6,7},{7,8},{8,9},{9,10},{10,1... | collective-permute-start | bytes 196616 | tf_op jit(solution)/shard_map/ppermute | solution.py:82
  243.0 6.4 %collective-permute-start.27 = (bf16[8,4096]{1,0:T(8,128)(2,1)S(1)}, bf16[8,4096]{1,0:T(8,128)(2,1)S(1)}, u32[]{:S(2)}, u32[]{:S(2)}) collective-permute-start(bf16[8,4096]{1,0:T(8,128)(2,1)S(1)} %collective-permute-done.26), channel_id=1, source_target_pairs={{0,1},{1,2},{2,3},{3,4},{4,5},{5,6},{6,7},{7,8},{8,9},{9,10},{10,1... | collective-permute-start | bytes 196616 | tf_op jit(solution)/shard_map/ppermute | solution.py:82
  249.4 6.4 %collective-permute-start.28 = (bf16[8,4096]{1,0:T(8,128)(2,1)S(1)}, bf16[8,4096]{1,0:T(8,128)(2,1)S(1)}, u32[]{:S(2)}, u32[]{:S(2)}) collective-permute-start(bf16[8,4096]{1,0:T(8,128)(2,1)S(1)} %collective-permute-done.27), channel_id=1, source_target_pairs={{0,1},{1,2},{2,3},{3,4},{4,5},{5,6},{6,7},{7,8},{8,9},{9,10},{10,1... | collective-permute-start | bytes 196616 | tf_op jit(solution)/shard_map/ppermute | solution.py:82
  255.7 6.4 %collective-permute-start.29 = (bf16[8,4096]{1,0:T(8,128)(2,1)S(1)}, bf16[8,4096]{1,0:T(8,128)(2,1)S(1)}, u32[]{:S(2)}, u32[]{:S(2)}) collective-permute-start(bf16[8,4096]{1,0:T(8,128)(2,1)S(1)} %collective-permute-done.28), channel_id=1, source_target_pairs={{0,1},{1,2},{2,3},{3,4},{4,5},{5,6},{6,7},{7,8},{8,9},{9,10},{10,1... | collective-permute-start | bytes 196616 | tf_op jit(solution)/shard_map/ppermute | solution.py:82
  262.1 6.4 %collective-permute-start.30 = (bf16[8,4096]{1,0:T(8,128)(2,1)S(1)}, bf16[8,4096]{1,0:T(8,128)(2,1)S(1)}, u32[]{:S(2)}, u32[]{:S(2)}) collective-permute-start(bf16[8,4096]{1,0:T(8,128)(2,1)S(1)} %collective-permute-done.29), channel_id=1, source_target_pairs={{0,1},{1,2},{2,3},{3,4},{4,5},{5,6},{6,7},{7,8},{8,9},{9,10},{10,1... | collective-permute-start | bytes 196616 | tf_op jit(solution)/shard_map/ppermute | solution.py:82
  (17 other events, 313.9 us)
Sparse Core Ops, SparseCore 0:
  110.8 55.2 reduce-scatter.2
  272.7 55.7 reduce-scatter.4
